TPU v7x, 512 devices: a whole 4x4x16 slice. The times are simulated.
512 devices in a mesh: row: 16 (over x, y), col: 32 (over z, core).
Axes of the slice: x: 4, y: 4, z: 16, core: 2. Of those that a mesh axis runs over, the one named last changes fastest.
Arguments:
- arrival: float32 [64, 16384], P(None, 'col'), may hold values from 0 to 4
- delay: bfloat16 [4, 16384, 16384], P(None, 'col', 'row'), may hold values from -40 to 20
- occupancy: int32 [4, 32, 32], replicated, may hold values from 0 to 1, as said below
Outputs:
- final_arrival: float32 [64, 16384], P(None, 'col')
- worst: float32 [64], replicated
Inputs may be any that keep to these rules, and one draw needn't show every extreme that they name: In every level every column of tiles holds at least one tile with occupancy 1.
All inputs are finite; a program needn't handle non-finite values.
Results may differ from a plain program's by a relative error of at most 0.0009.
Values sent between devices are 32-bit elements; how exact they have to be, the bound alone decides.
A program may use at most 64 MiB of HBM per device.

v0:
```python
import jax
import jax.numpy as jnp
from jax import lax
from jax.sharding import PartitionSpec as P


def from_everyone(shard, axis):
    copies = jnp.broadcast_to(shard, (lax.axis_size(axis), *shard.shape))
    return lax.all_to_all(copies, axis, split_axis=0, concat_axis=0, tiled=True)


def laid_out(tiles, dim):
    lengths = list(tiles.shape[1:])
    lengths[dim] *= tiles.shape[0]
    return jnp.moveaxis(tiles, 0, dim).reshape(lengths)


def gathered_copies(shard, axis, dim):
    tiles = from_everyone(shard, axis)
    return laid_out(tiles, dim)


def taken_together(shard, axis):
    return from_everyone(shard, axis).max(axis=0)


def level_max(times, delay_tile, keep):
    masked = jnp.where(keep[None, :], delay_tile.astype(jnp.float32), jnp.float32(-1000000000.0))
    rows = masked.shape[0]
    width = min(32, rows)
    turns = rows // width
    init = jnp.full((times.shape[0], masked.shape[1]), -1000000000.0, jnp.float32)

    def step(index, best):
        start = index * width
        part_a = lax.dynamic_slice_in_dim(times, start, width, 1)
        part_d = lax.dynamic_slice_in_dim(masked, start, width, 0)
        return jnp.maximum(best, jnp.max(part_a[:, :, None] + part_d[None, :, :], axis=1))

    return lax.fori_loop(0, turns, step, init)


def reduce_pieces(pieces):
    return jnp.max(pieces, axis=1)


def shards(arrival, delay, occupancy):
    col_count = lax.axis_size("col")
    row_count = lax.axis_size("row")
    ratio = col_count // row_count
    tile = arrival.shape[1]
    scenarios = arrival.shape[0]
    col_place = lax.axis_index("col")
    row_place = lax.axis_index("row")
    slice_pins = tile // row_count
    times = arrival
    for level in range(delay.shape[0]):
        flags = lax.dynamic_slice(occupancy[level], (col_place, row_place * ratio), (1, ratio))[0]
        keep = jnp.repeat(flags > 0, tile)
        partial_value = level_max(times, delay[level], keep)
        shaped = partial_value.reshape(scenarios, col_count, slice_pins)
        reduced = reduce_pieces(
            lax.all_to_all(shaped, "col", split_axis=1, concat_axis=1, tiled=True)
        )
        gathered = gathered_copies(reduced[None], "row", 0)
        outgoing = jnp.repeat(gathered, ratio, axis=0)
        arrived = lax.all_to_all(outgoing, "col", split_axis=0, concat_axis=0, tiled=True)
        start = col_place % ratio * row_count
        mine = lax.dynamic_slice_in_dim(arrived, start, row_count, 0)
        times = jnp.transpose(mine, (1, 0, 2)).reshape(scenarios, tile)
    worst = taken_together(jnp.max(times, axis=1), "col")
    return (times, worst)


def solution(mesh):
    placed = (P(None, "col"), P(None, "col", "row"), P())
    return jax.shard_map(
        shards, mesh=mesh, in_specs=placed, out_specs=(P(None, "col"), P()), check_vma=False
    )
```

profile of v0, /device:TPU:1, one launch (start us, length us, event | category | flops | bytes accessed | tf_op | source)
XLA Modules:
  0.0 488.1 jit_solution(14964154743765826624)
XLA Ops:
  2.0 5.4 %convert_select_fusion = (f32[512,1024]{1,0:T(8,128)S(1)}, f32[512,1024]{1,0:T(8,128)}, f32[512,1024]{1,0:T(8,128)}, f32[512,1024]{1,0:T(8,128)}) fusion(bf16[4,512,1024]{2,1,0:T(8,128)(2,1)} %param.12, pred[1024]{0:T(1024)(128)(4,1)S(1)} %broadcast_in_dim.122, pred[1024]{0:T(1024)(128)(4,1)S(1)} %broadcast_in_dim.112, ...), kind=kLoop, calls=%fused_computation.16 | loop fusion | flops 4194304 | bytes 12587008 | tf_op jit(solution)/shard_map/jit(_where)/select_n | solution.py:28
  7.4 55.0 %while.56 = (s32[]{:T(128)}, f32[64,1024]{1,0:T(8,128)S(1)}, f32[64,512]{1,0:T(8,128)}, f32[512,1024]{1,0:T(8,128)}, s32[]{:T(128)}, /*index=5*/s32[]{:T(128)}, s32[]{:T(128)}, s32[]{:T(128)}) while((s32[]{:T(128)}, f32[64,1024]{1,0:T(8,128)S(1)}, f32[64,512]{1,0:T(8,128)}, f32[512,1024]{1,0:T(8,128)}, s32[]{:T(128)}, ...), condition=%wide.region_2.3_spmd.clone, body=%wide.region_0.2_spmd.clone.sunk | while | flops 4259847 | bytes 1466517 | solution.py:40
  9.1 1.6 add_reduce_fusion.8
  12.5 1.6 add_reduce_fusion.8
  16.0 1.6 add_reduce_fusion.8
  19.4 1.6 add_reduce_fusion.8
  22.9 1.6 add_reduce_fusion.8
  26.3 1.6 add_reduce_fusion.8
  29.7 1.6 add_reduce_fusion.8
  33.2 1.6 add_reduce_fusion.8
  36.6 1.6 add_reduce_fusion.8
  40.1 1.6 add_reduce_fusion.8
  62.9 38.8 %all_to_all.66 = f32[32,1,2048]{2,1,0:T(1,128)S(1)} all-to-all(f32[32,1,2048]{2,1,0:T(1,128)S(1)} %reshape.112), channel_id=1, replica_groups=mesh['row'=16,'col'=32] {'col'}, dimensions={0} | all-to-all | bytes 524288 | tf_op jit(solution)/shard_map/all_to_all | solution.py:63
  104.0 13.4 %all_to_all.67 = f32[16,1,2048]{2,1,0:T(1,128)S(1)} all-to-all(f32[16,1,2048]{2,1,0:T(1,128)S(1)} %reshape.114), channel_id=1, replica_groups=mesh['row'=16,'col'=32] {'row'}, dimensions={0} | all-to-all | bytes 262144 | tf_op jit(solution)/shard_map/all_to_all | solution.py:9
  119.5 5.5 %all-to-all-start.2 = ((f32[32,1,2048]{2,1,0:T(1,128)}), f32[32,1,2048]{2,1,0:T(1,128)S(1)}, u32[]{:S(2)}, u32[]{:S(2)}) async-start(f32[32,1,2048]{2,1,0:T(1,128)} %reshape.116), calls=%async_computation.2 | async-start | bytes 524288 | tf_op jit(solution)/shard_map/all_to_all | solution.py:67
  125.0 21.6 %all-to-all-done.2 = f32[32,1,2048]{2,1,0:T(1,128)S(1)} async-done(((f32[32,1,2048]{2,1,0:T(1,128)}), f32[32,1,2048]{2,1,0:T(1,128)S(1)}, u32[]{:S(2)}, u32[]{:S(2)}) %all-to-all-start.2) | async-done | bytes 262176 | tf_op jit(solution)/shard_map/all_to_all | solution.py:67
  148.1 42.9 %while.57 = (s32[]{:T(128)}, f32[64,1024]{1,0:T(8,128)S(1)}, f32[64,512]{0,1:T(8,128)S(1)}, f32[512,1024]{1,0:T(8,128)}, s32[]{:T(128)}, /*index=5*/s32[]{:T(128)}, s32[]{:T(128)}, s32[]{:T(128)}) while((s32[]{:T(128)}, f32[64,1024]{1,0:T(8,128)S(1)}, f32[64,512]{0,1:T(8,128)S(1)}, f32[512,1024]{1,0:T(8,128)}, s32[]{:T(128)}, ...), condition=%wide.region_6.7_spmd.clone, body=%wide.region_4.6_spmd.clone.sunk | while | flops 4259847 | bytes 1482901 | solution.py:40
  191.6 25.8 %all_to_all.68 = f32[32,1,2048]{2,1,0:T(1,128)S(1)} all-to-all(f32[32,1,2048]{2,1,0:T(1,128)S(1)} %reshape.118), channel_id=1, replica_groups=mesh['row'=16,'col'=32] {'col'}, dimensions={0} | all-to-all | bytes 524288 | tf_op jit(solution)/shard_map/all_to_all | solution.py:63
  219.1 9.9 %all_to_all.69 = f32[16,1,2048]{2,1,0:T(1,128)S(1)} all-to-all(f32[16,1,2048]{2,1,0:T(1,128)S(1)} %reshape.120), channel_id=1, replica_groups=mesh['row'=16,'col'=32] {'row'}, dimensions={0} | all-to-all | bytes 262144 | tf_op jit(solution)/shard_map/all_to_all | solution.py:9
  231.2 6.5 %all-to-all-start.5 = ((f32[32,1,2048]{2,1,0:T(1,128)}), f32[32,1,2048]{2,1,0:T(1,128)S(1)}, u32[]{:S(2)}, u32[]{:S(2)}) async-start(f32[32,1,2048]{2,1,0:T(1,128)} %reshape.122), calls=%async_computation.5 | async-start | bytes 524288 | tf_op jit(solution)/shard_map/all_to_all | solution.py:67
  237.7 21.6 %all-to-all-done.5 = f32[32,1,2048]{2,1,0:T(1,128)S(1)} async-done(((f32[32,1,2048]{2,1,0:T(1,128)}), f32[32,1,2048]{2,1,0:T(1,128)S(1)}, u32[]{:S(2)}, u32[]{:S(2)}) %all-to-all-start.5) | async-done | bytes 262176 | tf_op jit(solution)/shard_map/all_to_all | solution.py:67
  260.9 42.9 %while.58 = (s32[]{:T(128)}, f32[64,1024]{1,0:T(8,128)S(1)}, f32[64,512]{0,1:T(8,128)S(1)}, f32[512,1024]{1,0:T(8,128)}, s32[]{:T(128)}, /*index=5*/s32[]{:T(128)}, s32[]{:T(128)}, s32[]{:T(128)}) while((s32[]{:T(128)}, f32[64,1024]{1,0:T(8,128)S(1)}, f32[64,512]{0,1:T(8,128)S(1)}, f32[512,1024]{1,0:T(8,128)}, s32[]{:T(128)}, ...), condition=%wide.region_10.11_spmd.clone, body=%wide.region_8.10_spmd.clone.sunk | while | flops 4259847 | bytes 1482901 | solution.py:40
  304.3 25.8 %all_to_all.70 = f32[32,1,2048]{2,1,0:T(1,128)S(1)} all-to-all(f32[32,1,2048]{2,1,0:T(1,128)S(1)} %reshape.124), channel_id=1, replica_groups=mesh['row'=16,'col'=32] {'col'}, dimensions={0} | all-to-all | bytes 524288 | tf_op jit(solution)/shard_map/all_to_all | solution.py:63
  331.8 9.9 %all_to_all.71 = f32[16,1,2048]{2,1,0:T(1,128)S(1)} all-to-all(f32[16,1,2048]{2,1,0:T(1,128)S(1)} %reshape.126), channel_id=1, replica_groups=mesh['row'=16,'col'=32] {'row'}, dimensions={0} | all-to-all | bytes 262144 | tf_op jit(solution)/shard_map/all_to_all | solution.py:9
  343.9 6.4 %all-to-all-start.8 = ((f32[32,1,2048]{2,1,0:T(1,128)}), f32[32,1,2048]{2,1,0:T(1,128)S(1)}, u32[]{:S(2)}, u32[]{:S(2)}) async-start(f32[32,1,2048]{2,1,0:T(1,128)} %reshape.128), calls=%async_computation.8 | async-start | bytes 524288 | tf_op jit(solution)/shard_map/all_to_all | solution.py:67
  350.3 21.6 %all-to-all-done.8 = f32[32,1,2048]{2,1,0:T(1,128)S(1)} async-done(((f32[32,1,2048]{2,1,0:T(1,128)}), f32[32,1,2048]{2,1,0:T(1,128)S(1)}, u32[]{:S(2)}, u32[]{:S(2)}) %all-to-all-start.8) | async-done | bytes 262176 | tf_op jit(solution)/shard_map/all_to_all | solution.py:67
  373.4 28.5 %while.59 = (s32[]{:T(128)}, f32[64,1024]{1,0:T(8,128)S(1)}, f32[64,512]{0,1:T(8,128)S(1)}, f32[512,1024]{1,0:T(8,128)S(1)}, s32[]{:T(128)}, /*index=5*/s32[]{:T(128)}, s32[]{:T(128)}, s32[]{:T(128)}) while((s32[]{:T(128)}, f32[64,1024]{1,0:T(8,128)S(1)}, f32[64,512]{0,1:T(8,128)S(1)}, f32[512,1024]{1,0:T(8,128)S(1)}, ...), condition=%wide.region_14.15_spmd.clone, body=%wide.region_12.14_spmd.clone.sunk | while | flops 4259847 | bytes 1482901 | solution.py:40
  402.5 25.8 %all_to_all.72 = f32[32,1,2048]{2,1,0:T(1,128)S(1)} all-to-all(f32[32,1,2048]{2,1,0:T(1,128)S(1)} %reshape.130), channel_id=1, replica_groups=mesh['row'=16,'col'=32] {'col'}, dimensions={0} | all-to-all | bytes 524288 | tf_op jit(solution)/shard_map/all_to_all | solution.py:63
  430.0 9.9 %all_to_all.73 = f32[16,1,2048]{2,1,0:T(1,128)S(1)} all-to-all(f32[16,1,2048]{2,1,0:T(1,128)S(1)} %reshape.132), channel_id=1, replica_groups=mesh['row'=16,'col'=32] {'row'}, dimensions={0} | all-to-all | bytes 262144 | tf_op jit(solution)/shard_map/all_to_all | solution.py:9
  441.4 27.1 %all_to_all.74 = f32[32,1,2048]{2,1,0:T(1,128)S(1)} all-to-all(f32[32,1,2048]{2,1,0:T(1,128)S(1)} %reshape.134), channel_id=1, replica_groups=mesh['row'=16,'col'=32] {'col'}, dimensions={0} | all-to-all | bytes 524288 | tf_op jit(solution)/shard_map/all_to_all | solution.py:67
  470.7 5.0 %all-to-all-start.12 = ((f32[32,1,64]{2,1,0:T(1,128)}), f32[32,1,64]{2,1,0:T(1,128)S(1)}, u32[]{:S(2)}, u32[]{:S(2)}) async-start(f32[32,1,64]{2,1,0:T(1,128)} %broadcast_in_dim.126), calls=%async_computation.12 | async-start | bytes 32768 | tf_op jit(solution)/shard_map/all_to_all | solution.py:9
  476.4 11.1 %all-to-all-done.12 = f32[32,1,64]{2,1,0:T(1,128)S(1)} async-done(((f32[32,1,64]{2,1,0:T(1,128)}), f32[32,1,64]{2,1,0:T(1,128)S(1)}, u32[]{:S(2)}, u32[]{:S(2)}) %all-to-all-start.12) | async-done | bytes 8224 | tf_op jit(solution)/shard_map/all_to_all | solution.py:9
  (373 shorter events, 177.1 us)
Async XLA Ops:
  119.5 27.1 %all-to-all-start.2 = ((f32[32,1,2048]{2,1,0:T(1,128)}), f32[32,1,2048]{2,1,0:T(1,128)S(1)}, u32[]{:S(2)}, u32[]{:S(2)}) async-start(f32[32,1,2048]{2,1,0:T(1,128)} %reshape.116), calls=%async_computation.2 | async-start | bytes 524288 | tf_op jit(solution)/shard_map/all_to_all | solution.py:67
  231.2 28.2 %all-to-all-start.5 = ((f32[32,1,2048]{2,1,0:T(1,128)}), f32[32,1,2048]{2,1,0:T(1,128)S(1)}, u32[]{:S(2)}, u32[]{:S(2)}) async-start(f32[32,1,2048]{2,1,0:T(1,128)} %reshape.122), calls=%async_computation.5 | async-start | bytes 524288 | tf_op jit(solution)/shard_map/all_to_all | solution.py:67
  343.9 28.0 %all-to-all-start.8 = ((f32[32,1,2048]{2,1,0:T(1,128)}), f32[32,1,2048]{2,1,0:T(1,128)S(1)}, u32[]{:S(2)}, u32[]{:S(2)}) async-start(f32[32,1,2048]{2,1,0:T(1,128)} %reshape.128), calls=%async_computation.8 | async-start | bytes 524288 | tf_op jit(solution)/shard_map/all_to_all | solution.py:67
  470.7 16.9 %all-to-all-start.12 = ((f32[32,1,64]{2,1,0:T(1,128)}), f32[32,1,64]{2,1,0:T(1,128)S(1)}, u32[]{:S(2)}, u32[]{:S(2)}) async-start(f32[32,1,64]{2,1,0:T(1,128)} %broadcast_in_dim.126), calls=%async_computation.12 | async-start | bytes 32768 | tf_op jit(solution)/shard_map/all_to_all | solution.py:9
where the time goes:
time: 491 us; the launch traced here: 488 us
  blocking collectives  186 us (38%)
  other arithmetic  124 us (25%)
  waiting for transfers between devices  76 us (15%)
  local copies, waits for them, and re-layouts  74 us (15%)
  starting transfers between devices  23.4 us (5%)
    all_to_all x4, blocking collectives, shards(): lax.all_to_all(shaped, 'col', split_axis=1, concat_axis=1, tiled=True)  116 us
    reduce_max x64, other arithmetic, step(): jnp.max(part_a[:, :, None] + part_d[None, :, :], axis=1)  98.3 us
    all_to_all x3, waiting for transfers between devices, shards(): lax.all_to_all(outgoing, 'col', split_axis=0, concat_axis=0, tiled=True)  64.9 us
    dynamic_slice x64, local copies, waits for them, and re-layouts, step(): part_d = lax.dynamic_slice_in_dim(masked, start, width, 0)  44.4 us
    all_to_all x4, blocking collectives, from_everyone(): return lax.all_to_all(copies, axis, split_axis=0, concat_axis=0, tiled=True)  43.1 us
    all_to_all x1, blocking collectives, shards(): lax.all_to_all(outgoing, 'col', split_axis=0, concat_axis=0, tiled=True)  27.1 us
    all_to_all x3, starting transfers between devices, shards(): lax.all_to_all(outgoing, 'col', split_axis=0, concat_axis=0, tiled=True)  18.4 us
    dynamic_slice x112, local copies, waits for them, and re-layouts, step(): part_a = lax.dynamic_slice_in_dim(times, start, width, 1)  17.8 us
  transfers between devices with their start and end apart: 4, of which 4 were waited for; matrix products, arithmetic and copies ran while one was open for 0% of the time, Pallas kernels for 0%

commit v1 on v0

v1 whole, which is shorter than its diff:
```python
import functools

import jax
import jax.numpy as jnp
from jax import lax
from jax.experimental import pallas as pl
from jax.experimental.pallas import tpu as pltpu
from jax.sharding import PartitionSpec as P

MESH = pl.DeviceIdType.MESH
NEG = -1000000000.0
GROUPS = 4
OWNERS = 4
LATE = 1
EARLY = 2


def kernel(
    arrival_ref, occ_ref, delay_ref,
    final_ref, worst_ref,
    raw, dmat, part, inbox, times, wbox, wown,
    raw_sem, part_send, part_recv, gath_send, gath_recv, w_send, w_recv,
):
    levels, tile, width = delay_ref.shape
    row = lax.axis_index("row")
    col = lax.axis_index("col")
    plane = col // 2
    core = lax.rem(col, 2)
    rows = 16
    cols = 32
    ups = times.shape[3]
    side = rows // OWNERS
    lane_tiles = tile // 128
    is_owner = lax.rem(row, side) == lax.rem(plane, side)
    is_root = row == plane
    slot = row // side

    fetches = [
        pltpu.make_async_copy(delay_ref.at[k], raw.at[k], raw_sem.at[k]) for k in range(levels)
    ]
    for fetch in fetches:
        fetch.start()

    barrier = pltpu.get_barrier_semaphore()

    def greet(to_row, to_col):
        @pl.when(jnp.logical_or(to_row != row, to_col != col))
        def _():
            pl.semaphore_signal(
                barrier, inc=1, device_id={"row": to_row, "col": to_col}, device_id_type=MESH
            )

    @pl.loop(0, 2 * OWNERS)
    def _(n):
        greet((n // 2) * side + lax.rem(row, side), 2 * row + lax.rem(n, 2))

    @pl.when(is_owner)
    def _():
        @pl.loop(0, cols)
        def _(n):
            greet(plane, n)

    @pl.loop(0, rows)
    def _(n):
        greet(n, col)

    @pl.loop(0, cols)
    def _(n):
        greet(row, n)

    def meet():
        extra = jnp.where(is_owner, jnp.where(is_root, cols - 2, cols), 0)
        pl.semaphore_wait(barrier, rows - 1 + cols - 1 + 2 * OWNERS + extra)

    def load_arrival():
        for g in range(GROUPS):
            for l in range(lane_tiles):
                for u in range(ups):
                    s = (g * ups + u) * 8
                    times[0, g, l, u] = arrival_ref[s : s + 8, l * 128 : (l + 1) * 128]

    def decode(k):
        pltpu.make_async_copy(delay_ref.at[k], raw.at[k], raw_sem.at[k]).wait()
        for h in range(2):
            keep = occ_ref[k, col, 2 * row + h] > 0

            @pl.loop(0, tile // 32)
            def _(n):
                at = pl.ds(pl.multiple_of(n * 32, 32), 32)
                for j in range(lane_tiles):
                    lanes = pl.ds(h * tile + j * 128, 128)
                    value = raw[k, at, lanes].astype(jnp.float32)
                    dmat[lax.rem(k, 2), h, j, at, :] = jnp.where(keep, value, jnp.float32(NEG))

    def send_part(k, g, h):
        @pl.when(jnp.logical_and(is_root, h == core))
        def _():
            inbox[k, g, col] = part[k, g, h, slot]

        @pl.loop(0, OWNERS)
        def _(o):
            to_row = o * side + lax.rem(row, side)
            to_col = 2 * row + h

            @pl.when(jnp.logical_or(to_row != row, to_col != col))
            def _():
                pltpu.make_async_remote_copy(
                    src_ref=part.at[k, g, h, o],
                    dst_ref=inbox.at[k, g, col],
                    send_sem=part_send.at[k, g],
                    recv_sem=part_recv.at[k, g],
                    device_id={"row": to_row, "col": to_col},
                    device_id_type=MESH,
                ).start()

    def compute(k, g, send):
        here = lax.rem(k, 2)

        @pl.loop(0, 2)
        def _(h):
            def chunk(l, best):
                best = list(best)
                t = [times[k, g, l, u] for u in range(ups)]
                start = pl.multiple_of(l * 128, 128)
                for i in range(128):
                    d = [
                        dmat[here, h, j, pl.ds(start + i, 8, stride=0), :]
                        for j in range(lane_tiles)
                    ]
                    for u in range(ups):
                        wide = jnp.broadcast_to(t[u][:, i : i + 1], (8, 128))
                        for j in range(lane_tiles):
                            n = u * lane_tiles + j
                            best[n] = jnp.maximum(best[n], wide + d[j])
                return tuple(best)

            init = tuple(jnp.full((8, 128), NEG, jnp.float32) for _ in range(ups * lane_tiles))
            best = lax.fori_loop(0, lane_tiles, chunk, init)
            for u in range(ups):
                for j in range(lane_tiles):
                    part[k, g, h, j, u] = best[u * lane_tiles + j]
            if send:
                send_part(k, g, h)

    def wait_bytes(ref, sem):
        pltpu.make_async_copy(ref, ref, sem).wait()

    def combine(k, g):
        @pl.when(is_owner)
        def _():
            @pl.when(is_root)
            def _():
                wait_bytes(inbox.at[k, g, pl.ds(0, cols - 1)], part_recv.at[k, g])

            @pl.when(jnp.logical_not(is_root))
            def _():
                wait_bytes(inbox.at[k, g], part_recv.at[k, g])

            for u in range(ups):
                tiles = [inbox[k, g, c, u] for c in range(cols)]
                while len(tiles) > 1:
                    tiles = [jnp.maximum(a, b) for a, b in zip(tiles[::2], tiles[1::2])]
                times[k + 1, g, slot, u] = tiles[0]

            @pl.loop(0, rows)
            def _(p):
                @pl.when(p != row)
                def _():
                    pltpu.make_async_remote_copy(
                        src_ref=times.at[k + 1, g, slot],
                        dst_ref=times.at[k + 1, g, slot],
                        send_sem=gath_send.at[k, g],
                        recv_sem=gath_recv.at[k, g],
                        device_id={"row": p, "col": col},
                        device_id_type=MESH,
                    ).start()

    def take(k, g):
        @pl.when(is_owner)
        def _():
            wait_bytes(times.at[k + 1, g, pl.ds(0, OWNERS - 1)], gath_recv.at[k, g])

        @pl.when(jnp.logical_not(is_owner))
        def _():
            wait_bytes(times.at[k + 1, g], gath_recv.at[k, g])

    load_arrival()
    decode(0)

    @pl.loop(0, EARLY)
    def _(g):
        compute(0, g, False)

    meet()

    @pl.loop(0, EARLY)
    def _(g):
        for h in range(2):
            send_part(0, g, h)

    @pl.loop(0, levels)
    def _(k):
        for g in range(GROUPS):
            @pl.when(k > 0)
            def _():
                if g == 0:
                    for n in range(GROUPS - LATE):
                        combine(k - 1, n)
                elif g <= LATE:
                    combine(k - 1, GROUPS - LATE + g - 1)
                take(k - 1, g)

            if g < EARLY:
                @pl.when(k > 0)
                def _():
                    compute(k, g, True)
            else:
                compute(k, g, True)

        @pl.when(k + 1 < levels)
        def _():
            decode(k + 1)

    for g in range(GROUPS):
        combine(levels - 1, g)
    lane = lax.broadcasted_iota(jnp.int32, (8, 128), 1)
    sub = lax.broadcasted_iota(jnp.int32, (8, 128), 0)
    low = jnp.float32(-3e38)
    spread = jnp.full((8, 128), low, jnp.float32)
    for g in range(GROUPS):
        take(levels - 1, g)
        for u in range(ups):
            n = g * ups + u
            s = n * 8
            tiles = [times[levels, g, l, u] for l in range(lane_tiles)]
            for l in range(lane_tiles):
                final_ref[s : s + 8, l * 128 : (l + 1) * 128] = tiles[l]
            top = functools.reduce(jnp.maximum, tiles)
            top = jnp.max(top, axis=1, keepdims=True)
            spread = jnp.where(lane // 8 == n, top, spread)
    spread = jnp.where(lax.rem(lane, 8) == sub, spread, low)
    spread = jnp.broadcast_to(jnp.max(spread, axis=0, keepdims=True), (8, 128))
    wown[...] = spread
    wbox[col] = spread

    @pl.loop(0, cols)
    def _(n):
        @pl.when(n != col)
        def _():
            pltpu.make_async_remote_copy(
                src_ref=wown,
                dst_ref=wbox.at[col],
                send_sem=w_send,
                recv_sem=w_recv,
                device_id={"row": row, "col": n},
                device_id_type=MESH,
            ).start()

    wait_bytes(wbox.at[pl.ds(0, cols - 1)], w_recv)
    tiles = [wbox[c] for c in range(cols)]
    worst_ref[...] = functools.reduce(jnp.maximum, tiles)

    wait_bytes(wbox.at[pl.ds(0, cols - 1)], w_send)

    @pl.loop(0, levels)
    def _(k):
        for g in range(GROUPS):
            @pl.when(is_root)
            def _():
                wait_bytes(inbox.at[k, g, pl.ds(0, 2 * OWNERS - 1)], part_send.at[k, g])

            @pl.when(jnp.logical_not(is_root))
            def _():
                wait_bytes(inbox.at[k, g, pl.ds(0, 2 * OWNERS)], part_send.at[k, g])

            @pl.when(is_owner)
            def _():
                wait_bytes(inbox.at[k, g, pl.ds(0, rows - 1)], gath_send.at[k, g])


def shards(arrival, delay, occupancy):
    levels, tile, width = delay.shape
    scenarios = arrival.shape[0]
    ups = scenarios // 8 // GROUPS
    lane_tiles = tile // 128
    cols = 32
    vmem = pl.BlockSpec(memory_space=pltpu.VMEM)
    final, worst = pl.pallas_call(
        kernel,
        out_shape=(
            jax.ShapeDtypeStruct((scenarios, tile), jnp.float32),
            jax.ShapeDtypeStruct((8, 128), jnp.float32),
        ),
        in_specs=[vmem, pl.BlockSpec(memory_space=pltpu.SMEM), pl.BlockSpec(memory_space=pl.ANY)],
        out_specs=(vmem, vmem),
        scratch_shapes=[
            pltpu.VMEM((levels, tile, width), jnp.bfloat16),
            pltpu.VMEM((2, 2, lane_tiles, tile, 128), jnp.float32),
            pltpu.VMEM((levels, GROUPS, 2, lane_tiles, ups, 8, 128), jnp.float32),
            pltpu.VMEM((levels, GROUPS, cols, ups, 8, 128), jnp.float32),
            pltpu.VMEM((levels + 1, GROUPS, lane_tiles, ups, 8, 128), jnp.float32),
            pltpu.VMEM((cols, 8, 128), jnp.float32),
            pltpu.VMEM((8, 128), jnp.float32),
            pltpu.SemaphoreType.DMA((levels,)),
            pltpu.SemaphoreType.DMA((levels, GROUPS)),
            pltpu.SemaphoreType.DMA((levels, GROUPS)),
            pltpu.SemaphoreType.DMA((levels, GROUPS)),
            pltpu.SemaphoreType.DMA((levels, GROUPS)),
            pltpu.SemaphoreType.DMA,
            pltpu.SemaphoreType.DMA,
        ],
        compiler_params=pltpu.CompilerParams(collective_id=0, has_side_effects=True),
    )(arrival, occupancy, delay)
    return final, worst[0, :scenarios]


def solution(mesh):
    placed = (P(None, "col"), P(None, "col", "row"), P())
    return jax.shard_map(
        shards, mesh=mesh, in_specs=placed, out_specs=(P(None, "col"), P()), check_vma=False
    )
```

time: 491 us -> 247 us (0.50)
  Pallas kernels: 0 us -> 244 us
  blocking collectives: 186 us -> 0 us
  other arithmetic: 124 us -> 0 us
  waiting for transfers between devices: 76 us -> 0 us
  local copies, waits for them, and re-layouts: 74 us -> 2.76 us
  starting transfers between devices: 23.4 us -> 0 us
    pallas_call x0 -> x1, Pallas kernels: none -> 244 us  [shards(): pl.pallas_call(kernel, out_shape=(jax.ShapeDtypeStruct((scenarios, tile),...]
    all_to_all x9 -> x0, blocking collectives: 186 us -> none  [the longest x4 116 us: shards(): lax.all_to_all(shaped, 'col', split_axis=1, concat_axis=1, tiled=True)]
    reduce_max x70 -> x0, other arithmetic: 99.1 us -> none  [the longest x64 98.3 us: step(): jnp.max(part_a[:, :, None] + part_d[None, :, :], axis=1)]
    all_to_all x4 -> x0, waiting for transfers between devices: 76 us -> none  [the longest x3 64.9 us: shards(): lax.all_to_all(outgoing, 'col', split_axis=0, concat_axis=0, tiled=True)]
    dynamic_slice x179 -> x0, local copies, waits for them, and re-layouts: 62.2 us -> none  [the longest x64 44.4 us: step(): part_d = lax.dynamic_slice_in_dim(masked, start, width, 0)]
    all_to_all x4 -> x0, starting transfers between devices: 23.4 us -> none  [the longest x3 18.4 us: shards(): lax.all_to_all(outgoing, 'col', split_axis=0, concat_axis=0, tiled=True)]
    all_to_all x12 -> x0, other arithmetic: 13.9 us -> none  [the longest x4 5.03 us: shards(): lax.all_to_all(outgoing, 'col', split_axis=0, concat_axis=0, tiled=True)]
    unnamed x29 -> x1, local copies, waits for them, and re-layouts: 8.42 us -> 1.57 us
  transfers between devices with their start and end apart: 4 -> 0, of which waited for: 4 -> 0; matrix products, arithmetic and copies ran while one was open for 0% -> 0% of each run, Pallas kernels for 0% -> 0%
where the time goes in v1:
time: 247 us
  Pallas kernels  244 us (99%)
  local copies, waits for them, and re-layouts  2.76 us (1%)
    pallas_call x1, Pallas kernels, shards(): pl.pallas_call(kernel, out_shape=(jax.ShapeDtypeStruct((scenarios, tile),...  244 us

profile of v1, /device:TPU:1, one launch (start us, length us, event | category | flops | bytes accessed | tf_op | source)
XLA Modules:
  0.0 247.1 jit_solution(16097689286406175833)
XLA Ops:
  0.6 243.7 %shard_map.50 = (f32[64,512]{1,0:T(8,128)}, f32[8,128]{1,0:T(8,128)}) custom-call(f32[64,512]{1,0:T(8,128)} %arrival_ref.1, s32[4,32,32]{2,1,0:T(8,128)} %occ_ref.1, bf16[4,512,1024]{2,1,0:T(8,128)(2,1)} %delay_ref.1), custom_call_target="tpu_custom_call" | custom-call | tf_op jit(solution)/shard_map/pallas_call | solution.py:288
  244.3 1.2 slice_bitcast_fusion
  245.5 1.6 copy.6
